TPU v7x, 512 devices: a whole 4x8x8 slice. The times are simulated.
512 devices in a mesh: blk: 128 (over z_lo, y, x), freq: 4 (over z_hi, core).
Axes of the slice: x: 4, y: 8, z: 8 (z_hi: 2, z_lo: 4; z = z_hi * 4 + z_lo), core: 2. Of those that a mesh axis runs over, the one named last changes fastest.
Arguments:
- node_index: int32 [3, 16384], P(None, 'blk'), may hold values from 0 to 63
- emitters: int32 [64], replicated, may hold values from 0 to 16383
- admittance: float32 [2, 16384], P(None, 'blk'), may hold values from -3 to 3
- wavenumbers: float32 [4], P('freq'), may hold values from 20 to 60
Outputs:
- scattered: bfloat16 [4, 2, 64, 16384], P('freq', None, None, 'blk')
- gradient: float32 [16384], P('blk')
All inputs are finite; a program needn't handle non-finite values.
Results may differ from a plain program's by a relative error of at most 0.006.
Values may be sent and summed in bfloat16 or wider, within the bound.
No kernel may reach another device: no remote copies, remote signals or barrier semaphores. Data moves between devices by JAX's collectives and lax.ppermute only.
A program may use at most 64 MiB of HBM per device.

v0:
```python
import jax
import jax.numpy as jnp
from jax import lax
from jax.sharding import Mesh
from jax.sharding import PartitionSpec as P

GRID = 64
BLK = ("blk_0", "blk_1", "blk_2")
soften = 0.0025


def in_order(blocks, dim):
    blocks = jnp.moveaxis(blocks, 0, dim)
    shape = blocks.shape
    return blocks.reshape(*shape[:dim], shape[dim] * shape[dim + 1], *shape[dim + 2 :])


def all_blocks(value, axes, turns):
    blocks = value
    for k in turns:
        blocks = lax.all_gather(blocks, axes[k])
    done = turns[::-1]
    back = [done.index(k) for k in range(len(axes))]
    blocks = blocks.transpose(*back, *range(len(axes), blocks.ndim))
    return blocks.reshape(-1, *value.shape)


def gather_axes(value, axes, turns, dim):
    return in_order(all_blocks(value, axes, turns), dim)


def copy_for_each(value, axis):
    copies = jnp.broadcast_to(value, (lax.axis_size(axis), *value.shape))
    return lax.all_to_all(copies, axis, split_axis=0, concat_axis=0, tiled=True)


def taken_together(value, axis):
    return copy_for_each(value, axis).sum(axis=0)


def green_tile(row_places, col_places, wavenum, strength):
    separation = row_places[:, :, None] - col_places[:, None, :]
    radius = jnp.sqrt(jnp.sum(separation * separation, axis=0) + soften)
    amplitude = strength / radius
    phase_turn = wavenum * radius
    return jnp.stack([amplitude * jnp.cos(phase_turn), amplitude * jnp.sin(phase_turn)]).astype(
        jnp.bfloat16
    )


def apply_tile(tile_data, source):
    real_part = jnp.einsum(
        "tc,rc->tr", source[0], tile_data[0], preferred_element_type=jnp.float32
    ) - jnp.einsum("tc,rc->tr", source[1], tile_data[1], preferred_element_type=jnp.float32)
    imag_part = jnp.einsum(
        "tc,rc->tr", source[1], tile_data[0], preferred_element_type=jnp.float32
    ) + jnp.einsum("tc,rc->tr", source[0], tile_data[1], preferred_element_type=jnp.float32)
    return jnp.stack([real_part, imag_part])


def complex_scale(factor_pair, field_pair):
    factor_real = factor_pair[0][None, :]
    factor_imag = factor_pair[1][None, :]
    real_part = factor_real * field_pair[0] - factor_imag * field_pair[1]
    imag_part = factor_real * field_pair[1] + factor_imag * field_pair[0]
    return jnp.stack([real_part, imag_part])


def row_potential(places, own_places, wavenum, strength, block_count, row_count):
    group_blocks = 1
    for candidate in range(1, block_count + 1):
        if block_count % candidate == 0 and candidate * row_count <= 4096:
            group_blocks = candidate
    group_cols = group_blocks * row_count

    def make_tile(group_id):
        col_places = lax.dynamic_slice_in_dim(places, group_id * group_cols, group_cols, 1)
        return green_tile(own_places, col_places, wavenum, strength)

    tile_stack = lax.map(make_tile, jnp.arange(block_count // group_blocks, dtype=jnp.int32))
    tile_flat = jnp.transpose(tile_stack, (1, 2, 0, 3)).reshape(
        2, row_count, block_count * row_count
    )

    def potential(source, whole_source):
        if whole_source is None:
            whole_source = gather_axes(source, BLK, (0, 1, 2), 2)
        return apply_tile(tile_flat, whole_source)

    return potential


def local(node_index, emitters, admittance, wavenumbers):
    block_count = lax.axis_size(BLK)
    lane_count = lax.axis_size("freq")
    row_count = node_index.shape[1]
    node_count = block_count * row_count
    emitter_count = emitters.shape[0]
    own_block = lax.axis_index(BLK)
    every_index = lax.all_gather(node_index, BLK, axis=1, tiled=True)
    places = every_index.astype(jnp.float32) / GRID
    own_places = node_index.astype(jnp.float32) / GRID
    wavenum = wavenumbers[0]
    strength = float(node_count) ** (-0.5)
    emitter_places = places[:, emitters]
    incident_whole = green_tile(emitter_places, places, wavenum, 1.0)
    incident = lax.dynamic_slice_in_dim(incident_whole, own_block * row_count, row_count, 2)
    potential = row_potential(places, own_places, wavenum, strength, block_count, row_count)
    first_wave = potential(incident, incident_whole)
    weighted = complex_scale(admittance, first_wave).astype(jnp.bfloat16)
    second = potential(weighted, None)
    lane_terms = jnp.sum(first_wave[0] * second[0] - first_wave[1] * second[1], axis=0) / (
        lane_count * emitter_count
    )
    gradient = taken_together(lane_terms, "freq")
    return (second.astype(jnp.bfloat16)[None], gradient)


def solution(mesh):
    split = Mesh(
        mesh.devices.reshape(4, 8, 4, mesh.shape["freq"]), ("blk_0", "blk_1", "blk_2", "freq")
    )
    in_specs = (P(None, BLK), P(), P(None, BLK), P("freq"))
    out_specs = (P("freq", None, None, BLK), P(BLK))
    return jax.shard_map(local, mesh=split, in_specs=in_specs, out_specs=out_specs, check_vma=False)
```

profile of v0, /device:TPU:1, one launch (start us, length us, event | category | flops | bytes accessed | tf_op | source)
XLA Modules:
  0.0 678.0 jit_solution(9046614232390934011)
XLA Ops:
  8.7 366.5 %all_gather.19 = s32[3,16384]{0,1:T(8,128)S(1)} all-gather(s32[3,128]{0,1:T(8,128)S(1)} %copy.41), channel_id=1, replica_groups=mesh['blk_0'=4,'blk_1'=8,'blk_2'=4,'freq'=4] {'blk_0','blk_1','blk_2'}, dimensions={1}, use_global_device_ids=true | all-gather | bytes 198144 | tf_op jit(solution)/shard_map/all_gather | solution.py:100
  375.2 3.5 convert_multiply_fusion
  378.8 5.5 copy.43
  384.3 4.0 gather_fusion
  389.0 3.6 multiply_reduce_fusion.1
  392.5 68.6 %while.10 = (s32[]{:T(128)}, bf16[4,2,128,4096]{2,3,0,1:T(8,128)(2,1)}, f32[3,128]{1,0:T(4,128)S(1)}, s32[4]{0:T(128)S(1)}, f32[3,16384]{1,0:T(4,128)S(1)}, /*in...) while((s32[]{:T(128)}, bf16[4,2,128,4096]{2,3,0,1:T(8,128)(2,1)}, f32[3,128]{1,0:T(4,128)S(1)}, ...), condition=%wide.region_3.4_spmd, body=%wide.region_1.3_spmd.sunk | while | flops 8912902 | bytes 19023540 | solution.py:80
  394.6 8.9 %fusion.43 = (bf16[1,1,128,4096]{3,2,1,0:T(8,128)(2,1)S(1)}, bf16[1,1,128,4096]{3,2,1,0:T(8,128)(2,1)S(1)}) fusion(f32[]{:T(128)} %get-tuple-element.164, f32[128,4096]{1,0:T(8,128)S(1)} %multiply_reduce_fusion.3), kind=kLoop, calls=%fused_computation.7.clone.1 | loop fusion | flops 3670016 | bytes 4194308 | tf_op jit(solution)/shard_map/while/body/eval_jaxpr/stack | solution.py:46
  405.1 3.1 copy.77
  411.8 8.9 %fusion.43 = (bf16[1,1,128,4096]{3,2,1,0:T(8,128)(2,1)S(1)}, bf16[1,1,128,4096]{3,2,1,0:T(8,128)(2,1)S(1)}) fusion(f32[]{:T(128)} %get-tuple-element.164, f32[128,4096]{1,0:T(8,128)S(1)} %multiply_reduce_fusion.3), kind=kLoop, calls=%fused_computation.7.clone.1 | loop fusion | flops 3670016 | bytes 4194308 | tf_op jit(solution)/shard_map/while/body/eval_jaxpr/stack | solution.py:46
  422.2 3.1 copy.77
  428.9 8.9 %fusion.43 = (bf16[1,1,128,4096]{3,2,1,0:T(8,128)(2,1)S(1)}, bf16[1,1,128,4096]{3,2,1,0:T(8,128)(2,1)S(1)}) fusion(f32[]{:T(128)} %get-tuple-element.164, f32[128,4096]{1,0:T(8,128)S(1)} %multiply_reduce_fusion.3), kind=kLoop, calls=%fused_computation.7.clone.1 | loop fusion | flops 3670016 | bytes 4194308 | tf_op jit(solution)/shard_map/while/body/eval_jaxpr/stack | solution.py:46
  439.4 3.1 copy.77
  446.1 8.9 %fusion.43 = (bf16[1,1,128,4096]{3,2,1,0:T(8,128)(2,1)S(1)}, bf16[1,1,128,4096]{3,2,1,0:T(8,128)(2,1)S(1)}) fusion(f32[]{:T(128)} %get-tuple-element.164, f32[128,4096]{1,0:T(8,128)S(1)} %multiply_reduce_fusion.3), kind=kLoop, calls=%fused_computation.7.clone.1 | loop fusion | flops 3670016 | bytes 4194308 | tf_op jit(solution)/shard_map/while/body/eval_jaxpr/stack | solution.py:46
  456.6 3.1 copy.77
  461.2 3.9 fusion.24
  465.8 16.6 %multiply_convert_fusion.2 = (bf16[64,16384]{1,0:T(8,128)(2,1)S(1)}, bf16[64,16384]{1,0:T(8,128)(2,1)S(1)}) fusion(f32[64,16384]{1,0:T(8,128)S(1)} %copy-done.4, f32[]{:T(128)} %bitcast.66), kind=kLoop, calls=%fused_computation.13 | loop fusion | flops 7340032 | bytes 8388612 | tf_op jit(solution)/shard_map/slice | solution.py:54
  486.0 11.2 %all_gather.20 = bf16[4,2,64,128]{3,2,1,0:T(8,128)(2,1)} all-gather(bf16[1,2,64,128]{3,2,1,0:T(8,128)(2,1)S(1)} %pad_maximum_fusion.1), channel_id=1, replica_groups=mesh['blk_0'=4,'blk_1'=8,'blk_2'=4,'freq'=4] {'blk_0'}, dimensions={0}, use_global_device_ids=true | all-gather | bytes 163840 | tf_op jit(solution)/shard_map/all_gather | solution.py:21
  497.4 84.1 %all-gather.5.cloned.1.call-done = bf16[32,2,64,128]{3,2,1,0:T(8,128)(2,1)} async-done(((bf16[4,2,64,128]{3,2,1,0:T(8,128)(2,1)}), bf16[32,2,64,128]{3,2,1,0:T(8,128)(2,1)}) %all-gather.5.cloned.1.call-update) | async-done | bytes 1048592 | tf_op jit(solution)/shard_map/all_gather | solution.py:21
  581.6 59.3 %all-gather.7.cloned.1.call-done = bf16[32,4,2,64,128]{4,3,2,1,0:T(8,128)(2,1)} async-done(((bf16[8,4,2,64,128]{4,3,2,1,0:T(8,128)(2,1)}), bf16[32,4,2,64,128]{4,3,2,1,0:T(8,128)(2,1)}) %all-gather.7.cloned.1.call-update) | async-done | bytes 4194320 | tf_op jit(solution)/shard_map/all_gather | solution.py:21
  640.8 3.1 copy.46
  648.8 1.6 fusion.4
  651.7 1.6 fusion.16
  655.5 8.2 %all-to-all-start = ((f32[4,1,128]{2,1,0:T(1,128)}), f32[4,1,128]{2,1,0:T(1,128)S(1)}, u32[]{:S(2)}, u32[]{:S(2)}) async-start(f32[4,1,128]{2,1,0:T(1,128)} %broadcast_in_dim.18), calls=%async_computation | async-start | bytes 4096 | tf_op jit(solution)/shard_map/all_to_all | solution.py:34
  664.3 6.4 all-to-all-done
  (61 shorter events, 33.1 us)
Async XLA Ops:
  7.2 574.4 %all-gather.5.cloned.1.call-start = ((), (), s32[]{:S(2)}) async-start(), calls=%async_computation.1 | async-start | bytes 1179648 | tf_op jit(solution)/shard_map/all_gather | solution.py:21
  378.8 5.5 copy-start.6
  461.2 4.7 copy-start.4
  465.1 18.2 %copy-start.2 = (bf16[1,128,4,4096]{1,3,2,0:T(8,128)(2,1)}, bf16[1,128,4,4096]{1,3,2,0:T(8,128)(2,1)S(1)}, u32[]{:S(2)}) copy-start(bf16[1,128,4,4096]{1,3,2,0:T(8,128)(2,1)S(1)} %get-tuple-element.86) | copy-start | bytes 12582916
  465.1 20.0 %copy-start = (bf16[1,128,4,4096]{1,3,2,0:T(8,128)(2,1)}, bf16[1,128,4,4096]{1,3,2,0:T(8,128)(2,1)S(1)}, u32[]{:S(2)}) copy-start(bf16[1,128,4,4096]{1,3,2,0:T(8,128)(2,1)S(1)} %get-tuple-element.85) | copy-start | bytes 12582916
  485.1 0.9 copy-start.5
  497.2 143.6 %all-gather.7.cloned.1.call-start = ((), (), s32[]{:S(2)}) async-start(), calls=%async_computation.2 | async-start | bytes 5242880 | tf_op jit(solution)/shard_map/all_gather | solution.py:21
  645.0 2.2 copy-start.1
  646.3 2.4 copy-start.3
  655.5 15.2 %all-to-all-start = ((f32[4,1,128]{2,1,0:T(1,128)}), f32[4,1,128]{2,1,0:T(1,128)S(1)}, u32[]{:S(2)}, u32[]{:S(2)}) async-start(f32[4,1,128]{2,1,0:T(1,128)} %broadcast_in_dim.18), calls=%async_computation | async-start | bytes 4096 | tf_op jit(solution)/shard_map/all_to_all | solution.py:34
Sparse Core Ops, SparseCore 0:
  497.3 84.1 all-gather.4
  583.6 57.1 all-gather.6
where the time goes:
time: 679 us; the launch traced here: 678 us
  blocking collectives  378 us (56%)
  waiting for transfers between devices  150 us (22%)
  other arithmetic  70.8 us (10%)
  local copies, waits for them, and re-layouts  43.9 us (6%)
  between operations  14.9 us (2%)
  matrix products  9.75 us (1%)
  starting transfers between devices  8.47 us (1%)
    all_gather x1, blocking collectives, local(): every_index = lax.all_gather(node_index, BLK, axis=1, tiled=True)  367 us
    all_gather x2, waiting for transfers between devices, all_blocks(): blocks = lax.all_gather(blocks, axes[k])  143 us
    another operation x8, other arithmetic, green_tile(): jnp.stack([amplitude * jnp.cos(phase_turn), amplitude * jnp.sin(phase_tur...  41.8 us
    dynamic_update_slice x8, local copies, waits for them, and re-layouts, row_potential(): lax.map(make_tile, jnp.arange(block_count // group_blocks, dtype=jnp.int32))  18.3 us
    slice x1, other arithmetic, apply_tile(): source[1]  16.6 us
  transfers between devices with their start and end apart: 3, of which 3 were waited for; matrix products, arithmetic and copies ran while one was open for 0% of the time, Pallas kernels for 0%

commit v1 on v0

--- a/solution.py
+++ b/solution.py
@@ -97,7 +97,7 @@
     node_count = block_count * row_count
     emitter_count = emitters.shape[0]
     own_block = lax.axis_index(BLK)
-    every_index = lax.all_gather(node_index, BLK, axis=1, tiled=True)
+    every_index = jnp.concatenate(lax.all_gather(node_index, axis_name=BLK), axis=1)
     places = every_index.astype(jnp.float32) / GRID
     own_places = node_index.astype(jnp.float32) / GRID
     wavenum = wavenumbers[0]

time: 679 us -> 632 us (0.931)
  blocking collectives: 378 us -> 326 us
    all_gather x1, blocking collectives: 367 us -> 315 us  [local(): lax.all_gather(node_index, axis_name=BLK)]
where the time goes in v1:
time: 632 us; the launch traced here: 631 us
  blocking collectives  326 us (52%)
  waiting for transfers between devices  154 us (24%)
  other arithmetic  67.4 us (11%)
  local copies, waits for them, and re-layouts  48 us (8%)
  between operations  14.9 us (2%)
  matrix products  9.75 us (2%)
  starting transfers between devices  8.47 us (1%)
    all_gather x1, blocking collectives, local(): lax.all_gather(node_index, axis_name=BLK)  315 us
    all_gather x2, waiting for transfers between devices, all_blocks(): blocks = lax.all_gather(blocks, axes[k])  147 us
    another operation x8, other arithmetic, green_tile(): jnp.stack([amplitude * jnp.cos(phase_turn), amplitude * jnp.sin(phase_tur...  41.8 us
    dynamic_update_slice x8, local copies, waits for them, and re-layouts, row_potential(): lax.map(make_tile, jnp.arange(block_count // group_blocks, dtype=jnp.int32))  18.3 us
    slice x1, other arithmetic, apply_tile(): source[1]  16.6 us
  transfers between devices with their start and end apart: 3, of which 3 were waited for; matrix products, arithmetic and copies ran while one was open for 0% of the time, Pallas kernels for 0%

profile of v1, /device:TPU:1, one launch (start us, length us, event | category | flops | bytes accessed | tf_op | source)
XLA Modules:
  0.0 631.0 jit_solution(12522936445613019308)
XLA Ops:
  7.9 314.8 %all-gather.3 = s32[128,3,128]{2,1,0:T(4,128)S(1)} all-gather(s32[1,3,128]{2,1,0:T(4,128)} %bitcast.90), channel_id=2, replica_groups=mesh['blk_0'=4,'blk_1'=8,'blk_2'=4,'freq'=4] {'blk_0','blk_1','blk_2'}, dimensions={0}, use_global_device_ids=true | all-gather | bytes 198144 | tf_op jit(solution)/shard_map/all_gather | solution.py:100
  322.8 4.9 copy.41
  327.6 5.5 copy.43
  333.1 4.0 gather_fusion
  337.9 3.6 multiply_reduce_fusion.1
  341.4 68.6 %while.10 = (s32[]{:T(128)}, bf16[4,2,128,4096]{2,3,0,1:T(8,128)(2,1)}, f32[3,128]{1,0:T(4,128)S(1)}, s32[4]{0:T(128)S(1)}, f32[3,16384]{1,0:T(4,128)S(1)}, /*in...) while((s32[]{:T(128)}, bf16[4,2,128,4096]{2,3,0,1:T(8,128)(2,1)}, f32[3,128]{1,0:T(4,128)S(1)}, ...), condition=%wide.region_3.4_spmd, body=%wide.region_1.3_spmd.sunk | while | flops 8912902 | bytes 19023540 | solution.py:80
  343.5 8.9 %fusion.43 = (bf16[1,1,128,4096]{3,2,1,0:T(8,128)(2,1)S(1)}, bf16[1,1,128,4096]{3,2,1,0:T(8,128)(2,1)S(1)}) fusion(f32[]{:T(128)} %get-tuple-element.164, f32[128,4096]{1,0:T(8,128)S(1)} %multiply_reduce_fusion.3), kind=kLoop, calls=%fused_computation.7.clone.1 | loop fusion | flops 3670016 | bytes 4194308 | tf_op jit(solution)/shard_map/while/body/eval_jaxpr/stack | solution.py:46
  354.0 3.1 copy.77
  360.7 8.9 %fusion.43 = (bf16[1,1,128,4096]{3,2,1,0:T(8,128)(2,1)S(1)}, bf16[1,1,128,4096]{3,2,1,0:T(8,128)(2,1)S(1)}) fusion(f32[]{:T(128)} %get-tuple-element.164, f32[128,4096]{1,0:T(8,128)S(1)} %multiply_reduce_fusion.3), kind=kLoop, calls=%fused_computation.7.clone.1 | loop fusion | flops 3670016 | bytes 4194308 | tf_op jit(solution)/shard_map/while/body/eval_jaxpr/stack | solution.py:46
  371.1 3.1 copy.77
  377.8 8.9 %fusion.43 = (bf16[1,1,128,4096]{3,2,1,0:T(8,128)(2,1)S(1)}, bf16[1,1,128,4096]{3,2,1,0:T(8,128)(2,1)S(1)}) fusion(f32[]{:T(128)} %get-tuple-element.164, f32[128,4096]{1,0:T(8,128)S(1)} %multiply_reduce_fusion.3), kind=kLoop, calls=%fused_computation.7.clone.1 | loop fusion | flops 3670016 | bytes 4194308 | tf_op jit(solution)/shard_map/while/body/eval_jaxpr/stack | solution.py:46
  388.3 3.1 copy.77
  395.0 8.9 %fusion.43 = (bf16[1,1,128,4096]{3,2,1,0:T(8,128)(2,1)S(1)}, bf16[1,1,128,4096]{3,2,1,0:T(8,128)(2,1)S(1)}) fusion(f32[]{:T(128)} %get-tuple-element.164, f32[128,4096]{1,0:T(8,128)S(1)} %multiply_reduce_fusion.3), kind=kLoop, calls=%fused_computation.7.clone.1 | loop fusion | flops 3670016 | bytes 4194308 | tf_op jit(solution)/shard_map/while/body/eval_jaxpr/stack | solution.py:46
  405.4 3.1 copy.77
  410.1 3.9 fusion.24
  414.7 16.6 %multiply_convert_fusion.2 = (bf16[64,16384]{1,0:T(8,128)(2,1)S(1)}, bf16[64,16384]{1,0:T(8,128)(2,1)S(1)}) fusion(f32[64,16384]{1,0:T(8,128)S(1)} %copy-done.4, f32[]{:T(128)} %bitcast.70), kind=kLoop, calls=%fused_computation.12 | loop fusion | flops 7340032 | bytes 8388612 | tf_op jit(solution)/shard_map/slice | solution.py:54
  434.9 11.2 %all_gather.24 = bf16[4,2,64,128]{3,2,1,0:T(8,128)(2,1)} all-gather(bf16[1,2,64,128]{3,2,1,0:T(8,128)(2,1)S(1)} %pad_maximum_fusion.1), channel_id=1, replica_groups=mesh['blk_0'=4,'blk_1'=8,'blk_2'=4,'freq'=4] {'blk_0'}, dimensions={0}, use_global_device_ids=true | all-gather | bytes 163840 | tf_op jit(solution)/shard_map/all_gather | solution.py:21
  446.3 88.2 %all-gather.7.cloned.1.call-done = bf16[32,2,64,128]{3,2,1,0:T(8,128)(2,1)} async-done(((bf16[4,2,64,128]{3,2,1,0:T(8,128)(2,1)}), bf16[32,2,64,128]{3,2,1,0:T(8,128)(2,1)}) %all-gather.7.cloned.1.call-update) | async-done | bytes 1048592 | tf_op jit(solution)/shard_map/all_gather | solution.py:21
  534.5 59.3 %all-gather.9.cloned.1.call-done = bf16[32,4,2,64,128]{4,3,2,1,0:T(8,128)(2,1)} async-done(((bf16[8,4,2,64,128]{4,3,2,1,0:T(8,128)(2,1)}), bf16[32,4,2,64,128]{4,3,2,1,0:T(8,128)(2,1)}) %all-gather.9.cloned.1.call-update) | async-done | bytes 4194320 | tf_op jit(solution)/shard_map/all_gather | solution.py:21
  593.8 3.1 copy.46
  601.7 1.6 fusion.4
  604.7 1.6 fusion.16
  608.4 8.2 %all-to-all-start = ((f32[4,1,128]{2,1,0:T(1,128)}), f32[4,1,128]{2,1,0:T(1,128)S(1)}, u32[]{:S(2)}, u32[]{:S(2)}) async-start(f32[4,1,128]{2,1,0:T(1,128)} %broadcast_in_dim.18), calls=%async_computation | async-start | bytes 4096 | tf_op jit(solution)/shard_map/all_to_all | solution.py:34
  617.2 6.4 %all-to-all-done = f32[4,1,128]{2,1,0:T(1,128)S(1)} async-done(((f32[4,1,128]{2,1,0:T(1,128)}), f32[4,1,128]{2,1,0:T(1,128)S(1)}, u32[]{:S(2)}, u32[]{:S(2)}) %all-to-all-start) | async-done | bytes 2080 | tf_op jit(solution)/shard_map/all_to_all | solution.py:34
  (61 shorter events, 32.4 us)
Async XLA Ops:
  7.2 527.3 %all-gather.7.cloned.1.call-start = ((), (), s32[]{:S(2)}) async-start(), calls=%async_computation.1 | async-start | bytes 1179648 | tf_op jit(solution)/shard_map/all_gather | solution.py:21
  327.6 5.5 copy-start.6
  410.1 4.7 copy-start.4
  414.0 18.2 %copy-start.2 = (bf16[1,128,4,4096]{1,3,2,0:T(8,128)(2,1)}, bf16[1,128,4,4096]{1,3,2,0:T(8,128)(2,1)S(1)}, u32[]{:S(2)}) copy-start(bf16[1,128,4,4096]{1,3,2,0:T(8,128)(2,1)S(1)} %get-tuple-element.86) | copy-start | bytes 12582916
  414.0 20.0 %copy-start = (bf16[1,128,4,4096]{1,3,2,0:T(8,128)(2,1)}, bf16[1,128,4,4096]{1,3,2,0:T(8,128)(2,1)S(1)}, u32[]{:S(2)}) copy-start(bf16[1,128,4,4096]{1,3,2,0:T(8,128)(2,1)S(1)} %get-tuple-element.85) | copy-start | bytes 12582916
  434.0 0.9 copy-start.5
  446.1 147.7 %all-gather.9.cloned.1.call-start = ((), (), s32[]{:S(2)}) async-start(), calls=%async_computation.2 | async-start | bytes 5242880 | tf_op jit(solution)/shard_map/all_gather | solution.py:21
  597.9 2.2 copy-start.1
  599.3 2.4 copy-start.3
  608.4 15.2 %all-to-all-start = ((f32[4,1,128]{2,1,0:T(1,128)}), f32[4,1,128]{2,1,0:T(1,128)S(1)}, u32[]{:S(2)}, u32[]{:S(2)}) async-start(f32[4,1,128]{2,1,0:T(1,128)} %broadcast_in_dim.18), calls=%async_computation | async-start | bytes 4096 | tf_op jit(solution)/shard_map/all_to_all | solution.py:34
Sparse Core Ops, SparseCore 0:
  446.2 88.2 all-gather.6
  536.6 57.1 all-gather.8
